TPU v7x, 32 devices: a whole 2x2x4 slice. The times are simulated.
32 devices in a mesh: pts: 8 (over z, y), cent: 4 (over x, core).
Axes of the slice: x: 2, y: 2, z: 4, core: 2. Of those that a mesh axis runs over, the one named last changes fastest.
Arguments:
- points: bfloat16 [65536, 512], P(('pts', 'cent')), may hold values from -128 to 128
- centroids: bfloat16 [8192, 512], P('pts'), may hold values from -32 to 32
- candidates: int32 [4096, 2], P(('pts', 'cent')), may hold values from 0 to 31, all different within a row; in each aligned block of 128 rows (0 to 127, 128 to 255, ...) at most 9 rows name the same one
Outputs:
- new_centroids: bfloat16 [8192, 512], P('pts')
- point_lse: float32 [65536], P(('pts', 'cent'))
Inputs may be any that keep to these rules, and one draw needn't show every extreme that they name: `candidates`: within the 128 point blocks of one device, no centroid block is named more than 9 times; the two ids of a point block differ.
All inputs are finite; a program needn't handle non-finite values.
Results may differ from a plain program's by a relative error of at most 0.006.
Values may be sent and summed in bfloat16 or wider, within the bound.
A program may use at most 64 MiB of HBM per device.

v0:
```python
import math

import jax
import jax.numpy as jnp
from jax import lax
from jax.sharding import PartitionSpec as P

CB = 256
PB = 16
ITERS = 2


def stable_lse(scores, reduce_axis):
    highest = jnp.max(scores, axis=reduce_axis, keepdims=True)
    summed = jnp.sum(jnp.exp(scores - highest), axis=reduce_axis)
    return jnp.squeeze(highest, reduce_axis) + jnp.log(summed)


def make_scoring(centre_table, centre_norms, inverse_root):

    def scoring(package):
        slot_rows, slot_flags = package
        leading = slot_rows.shape[0]
        flat_rows = slot_rows.reshape(leading, -1, slot_rows.shape[-1])
        products = jnp.einsum(
            "lsd,lmd->lsm", flat_rows, centre_table, preferred_element_type=jnp.float32
        )
        scores = inverse_root * (2.0 * products - centre_norms[:, None, :])
        scores = scores.reshape(slot_rows.shape[:-1] + (centre_table.shape[1],))
        return (slot_rows, slot_flags, scores, stable_lse(scores, scores.ndim - 1))

    return scoring


def on_device(points, centroids, candidates):
    feature_width = points.shape[1]
    inverse_root = 1.0 / math.sqrt(feature_width)
    owners = lax.axis_size("pts")
    held_blocks = centroids.shape[0] // CB
    point_blocks = candidates.shape[0]
    total_blocks = held_blocks * owners
    capacity = max(2, 2 * point_blocks // total_blocks + 1)
    slot_count = held_blocks * owners * capacity
    grouped = points.reshape(point_blocks, PB, feature_width)
    picked = candidates.reshape(-1)
    entry_count = picked.shape[0]
    labels = jnp.arange(total_blocks, dtype=jnp.int32)
    member = (picked[:, None] == labels[None, :]).astype(jnp.bfloat16)
    entry_index = jnp.arange(entry_count, dtype=jnp.int32)
    earlier = (entry_index[None, :] < entry_index[:, None]).astype(jnp.bfloat16)
    prior_hits = jnp.dot(earlier, member, preferred_element_type=jnp.float32)
    arrival = jnp.sum(prior_hits * member.astype(jnp.float32), axis=1).astype(jnp.int32)
    local_block = picked % held_blocks
    target = picked // held_blocks
    position = (local_block * owners + target) * capacity + arrival
    slot_shape = (held_blocks, owners, capacity)
    current = centroids
    places = jnp.arange(slot_count, dtype=jnp.int32)
    source = (
        jnp.sum(
            jnp.where(position[:, None] == places[None, :], entry_index[:, None] + 1, 0), axis=0
        )
        - 1
    )
    filled = source >= 0
    home_block = jnp.maximum(source, 0) // 2
    outgoing = jnp.where(filled[:, None, None], grouped[home_block], jnp.zeros((), jnp.bfloat16))
    outgoing = outgoing.reshape(slot_shape + (PB, feature_width))
    slot_marks = jnp.broadcast_to(filled[:, None], (slot_count, PB)).astype(jnp.bfloat16)
    slot_marks = slot_marks.reshape(slot_shape + (PB,))
    point_lse = jnp.zeros((point_blocks, PB), jnp.float32)
    arrived = lax.all_to_all(outgoing, "pts", split_axis=1, concat_axis=1, tiled=True)
    arrived_marks = lax.all_to_all(slot_marks, "pts", split_axis=1, concat_axis=1, tiled=True)
    for iteration in range(ITERS):
        centre_table = current.reshape(-1, CB, feature_width)
        centre_norms = jnp.sum(jnp.square(centre_table.astype(jnp.float32)), axis=2)
        scoring = make_scoring(centre_table, centre_norms, inverse_root)
        arrived, arrived_marks, scores, partial_value = scoring(
            (arrived, arrived_marks)
        )
        returned = lax.all_to_all(partial_value, "pts", split_axis=1, concat_axis=1, tiled=True)
        per_entry = returned.reshape(slot_count, PB)[position]
        paired = per_entry.reshape(point_blocks, 2, PB)
        point_lse = stable_lse(paired, 1)
        outward = jnp.where(filled[:, None], point_lse[home_block], jnp.zeros((), jnp.float32))
        outward = outward.reshape(slot_shape + (PB,))
        inward = lax.all_to_all(outward, "pts", split_axis=1, concat_axis=1, tiled=True)
        weights = jnp.exp(scores - inward[..., None]) * arrived_marks.astype(jnp.float32)[..., None]
        leading = weights.shape[0]
        flat_weights = weights.reshape(leading, -1, CB)
        masses = jnp.sum(flat_weights, axis=1).reshape(leading * CB)
        rounded = flat_weights.astype(jnp.bfloat16)
        flat_rows = arrived.reshape(leading, -1, feature_width)
        weighted = jnp.einsum(
            "lsm,lsd->lmd", rounded, flat_rows, preferred_element_type=jnp.float32
        )
        weighted = weighted.reshape(leading * CB, feature_width)
        share_sums, share_mass = (
            lax.psum_scatter(weighted, "cent", scatter_dimension=0, tiled=True),
            lax.psum_scatter(masses, "cent", scatter_dimension=0, tiled=True),
        )
        share_rows = share_sums.shape[0]
        first_row = lax.axis_index("cent") * share_rows
        previous = lax.dynamic_slice_in_dim(current, first_row, share_rows, 0).astype(jnp.float32)
        renewed = ((share_sums + previous) / (share_mass[:, None] + 1.0)).astype(jnp.bfloat16)
        current = lax.all_gather(renewed, "cent", axis=0, tiled=True)
    return (current, point_lse.reshape(-1))


def solution(mesh):
    return jax.shard_map(
        on_device,
        mesh=mesh,
        in_specs=(P(("pts", "cent"), None), P("pts", None), P(("pts", "cent"), None)),
        out_specs=(P("pts", None), P(("pts", "cent"))),
        check_vma=False,
    )
```

profile of v0, /device:TPU:0, one launch (start us, length us, event | category | flops | bytes accessed | tf_op | source)
XLA Modules:
  0.0 339.6 jit_solution(14699359825490993864)
XLA Ops:
  7.2 0.9 copy.69
  8.8 13.3 %gather_fusion = bf16[288,16,512]{2,1,0:T(8,128)(2,1)} fusion(bf16[128,16,512]{2,1,0:T(8,128)(2,1)S(1)} %bitcast.41, s32[1024]{0:T(1024)S(1)} %pad_clamp_fusion.1), kind=kCustom, calls=%fused_computation | custom fusion | bytes 9438336 | tf_op jit(solution)/shard_map/gather | solution.py:67
  22.2 2.6 broadcast_select_fusion
  24.8 2.7 copy.70
  27.5 7.4 %all-to-all-start = ((bf16[4,8,9,16,512]{4,3,2,0,1:T(8,128)(2,1)}), bf16[4,8,9,16,512]{4,3,2,0,1:T(8,128)(2,1)}, u32[]{:S(2)}, u32[]{:S(2)}) async-start(bf16[4,8,9,16,512]{4,3,2,0,1:T(8,128)(2,1)} %copy.70), calls=%async_computation | async-start | bytes 9437184 | tf_op jit(solution)/shard_map/all_to_all | solution.py:72
  35.1 0.3 multiply_reduce_fusion.1
  35.7 0.7 reshape.400
  36.5 103.0 %all-to-all-done = bf16[4,8,9,16,512]{4,3,2,0,1:T(8,128)(2,1)} async-done(((bf16[4,8,9,16,512]{4,3,2,0,1:T(8,128)(2,1)}), bf16[4,8,9,16,512]{4,3,2,0,1:T(8,128)(2,1)}, u32[]{:S(2)}, u32[]{:S(2)}) %all-to-all-start) | async-done | bytes 4718624 | tf_op jit(solution)/shard_map/all_to_all | solution.py:72
  139.5 3.6 %all-to-all-start.3 = ((bf16[8,2,288]{2,1,0:T(2,128)(2,1)}), bf16[8,2,288]{2,1,0:T(2,128)(2,1)S(1)}, u32[]{:S(2)}, u32[]{:S(2)}) async-start(bf16[8,2,288]{2,1,0:T(2,128)(2,1)} %reshape.400), calls=%async_computation.3 | async-start | bytes 24576 | tf_op jit(solution)/shard_map/all_to_all | solution.py:73
  143.1 2.8 copy.71
  146.0 1.6 fusion.25
  147.6 0.5 copy-done.1
  148.1 2.2 copy-done.2
  150.3 0.6 exponential_reduce_fusion.1
  150.9 0.8 add.172
  151.8 1.0 copy.98
  152.8 0.8 reshape.402
  153.6 6.0 %all-to-all-start.1 = ((f32[8,1,576]{2,1,0:T(1,128)}), f32[8,1,576]{2,1,0:T(1,128)S(1)}, u32[]{:S(2)}, u32[]{:S(2)}) async-start(f32[8,1,576]{2,1,0:T(1,128)} %reshape.402), calls=%async_computation.1 | async-start | bytes 40960 | tf_op jit(solution)/shard_map/all_to_all | solution.py:81
  159.7 6.5 %all-to-all-done.1 = f32[8,1,576]{2,1,0:T(1,128)S(1)} async-done(((f32[8,1,576]{2,1,0:T(1,128)}), f32[8,1,576]{2,1,0:T(1,128)S(1)}, u32[]{:S(2)}, u32[]{:S(2)}) %all-to-all-start.1) | async-done | bytes 18464 | tf_op jit(solution)/shard_map/all_to_all | solution.py:81
  166.2 0.5 broadcast.360
  166.7 0.7 reduce.8
  167.5 0.7 copy.88
  168.2 1.0 reshape.392
  169.2 0.7 gather_fusion.1
  170.4 1.1 gather_fusion.2
  171.5 1.0 gather.25
  172.5 1.7 broadcast_select_fusion.2
  174.2 1.2 copy.77
  175.4 0.7 reshape.404
  176.2 3.3 all-to-all-start.2
  179.8 0.7 copy.81
  180.5 1.1 reshape.351
  181.6 4.5 %all-to-all-done.2 = f32[8,1,576]{2,1,0:T(1,128)S(1)} async-done(((f32[8,1,576]{2,1,0:T(1,128)}), f32[8,1,576]{2,1,0:T(1,128)S(1)}, u32[]{:S(2)}, u32[]{:S(2)}) %all-to-all-start.2) | async-done | bytes 18464 | tf_op jit(solution)/shard_map/all_to_all | solution.py:87
  186.1 0.7 reduce.9
  186.9 0.7 copy.78
  187.6 1.1 sub.105
  188.7 6.6 %fusion.10 = f32[4,256,512]{2,1,0:T(8,128)} fusion(bf16[4,1152,512]{2,1,0:T(8,128)(2,1)} %bitcast.43, f32[4,1152,256]{1,2,0:T(8,128)} %copy-done.2, f32[4,1152]{1,0:T(4,128)S(1)} %reshape.351, f32[4,1152]{1,0:T(4,128)S(1)} %sub.105), kind=kOutput, calls=%fused_computation.21 | convolution fusion | flops 1211498496 | bytes 11571200 | tf_op jit(solution)/shard_map/lsm,lsd->lmd/dot_general | solution.py:94
  195.4 0.6 dynamic-slice
  196.7 3.5 %fusion.4 = f32[4,256]{1,0:T(4,128)S(1)} fusion(f32[4,1152,256]{1,2,0:T(8,128)} %copy-done.2, f32[4,1152]{1,0:T(4,128)S(1)} %reshape.351, f32[4,1152]{1,0:T(4,128)S(1)} %sub.105), kind=kLoop, calls=%fused_computation.16 | loop fusion | flops 3537920 | bytes 4759552 | tf_op jit(solution)/shard_map/reduce_sum | solution.py:91
  200.2 5.7 %all-reduce = f32[1024]{0:T(1024)S(1)} all-reduce(f32[1024]{0:T(1024)S(1)} %bitcast.66), channel_id=3, replica_groups=mesh['pts'=8,'cent'=4] {'cent'}, use_global_device_ids=true, to_apply=%region_9.10.clone | all-reduce | flops 1024 | bytes 8192
  205.9 18.0 %reduce-scatter.3.cloned.1.call-done = f32[256,512]{1,0:T(8,128)} async-done(((f32[1024,512]{1,0:T(8,128)}), f32[256,512]{1,0:T(8,128)}) %reduce-scatter.3.cloned.1.call-update) | async-done | bytes 524304 | tf_op jit(solution)/shard_map/reduce_scatter | solution.py:99
  224.0 1.9 divide_convert_fusion.1
  225.9 16.9 %all-gather.3.cloned.1.call-done = bf16[1024,512]{1,0:T(8,128)(2,1)} async-done(((bf16[256,512]{1,0:T(8,128)(2,1)}), bf16[1024,512]{1,0:T(8,128)(2,1)}) %all-gather.3.cloned.1.call-update) | async-done | bytes 1048592 | tf_op jit(solution)/shard_map/all_gather | solution.py:106
  242.8 1.5 multiply_reduce_fusion
  244.3 4.2 %fusion.26 = (f32[4,1152]{1,0:T(4,128)S(1)}, f32[4,1152,256]{1,2,0:T(8,128)S(1)}) fusion(f32[4,256]{1,0:T(4,128)S(1)} %sub.108, bf16[4,1152,512]{2,1,0:T(8,128)(2,1)} %bitcast.44, bf16[4,256,512]{2,1,0:T(8,128)(2,1)} %bitcast.50), kind=kOutput, calls=%fused_computation.77 | convolution fusion | flops 1212673536 | bytes 10508288 | tf_op jit(solution)/shard_map/lsd,lmd->lsm/dot_general | solution.py:25
  248.6 2.2 copy-done.3
  250.8 0.6 exponential_reduce_fusion
  251.8 11.9 %all_to_all.30 = f32[8,1,576]{2,1,0:T(1,128)S(1)} all-to-all(f32[8,1,576]{2,1,0:T(1,128)S(1)} %reshape.406), channel_id=1, replica_groups=mesh['pts'=8,'cent'=4] {'pts'}, dimensions={0} | all-to-all | bytes 36864 | tf_op jit(solution)/shard_map/all_to_all | solution.py:81
  263.7 0.7 reduce.10
  264.6 0.7 gather_fusion.3
  265.5 0.2 exponential_reduce_fusion.2
  265.8 1.1 gather_fusion.4
  266.9 0.3 gather.28
  267.3 0.3 copy.86
  267.7 9.0 %all_to_all.31 = f32[8,1,576]{2,1,0:T(1,128)S(1)} all-to-all(f32[8,1,576]{2,1,0:T(1,128)S(1)} %reshape.408), channel_id=1, replica_groups=mesh['pts'=8,'cent'=4] {'pts'}, dimensions={0} | all-to-all | bytes 36864 | tf_op jit(solution)/shard_map/all_to_all | solution.py:87
  276.7 0.7 reduce.11
  277.7 6.6 %fusion.8 = f32[4,256,512]{2,1,0:T(8,128)} fusion(bf16[4,1152,512]{2,1,0:T(8,128)(2,1)} %bitcast.45, f32[4,1152,256]{1,2,0:T(8,128)} %copy-done.3, f32[4,1152]{1,0:T(4,128)S(1)} %sub.115, f32[4,1152]{1,0:T(4,128)S(1)} %reshape.351), kind=kOutput, calls=%fused_computation.20 | convolution fusion | flops 1211498496 | bytes 11571200 | tf_op jit(solution)/shard_map/lsm,lsd->lmd/dot_general | solution.py:94
  284.4 3.5 %fusion.6 = f32[4,256]{1,0:T(4,128)S(1)} fusion(f32[4,1152,256]{1,2,0:T(8,128)} %copy-done.3, f32[4,1152]{1,0:T(4,128)S(1)} %sub.115, f32[4,1152]{1,0:T(4,128)S(1)} %reshape.351), kind=kLoop, calls=%fused_computation.18 | loop fusion | flops 3537920 | bytes 4759552 | tf_op jit(solution)/shard_map/reduce_sum | solution.py:91
  287.9 5.8 %all-reduce.1 = f32[1024]{0:T(1024)S(1)} all-reduce(f32[1024]{0:T(1024)S(1)} %bitcast.67), channel_id=5, replica_groups=mesh['pts'=8,'cent'=4] {'cent'}, use_global_device_ids=true, to_apply=%region_17.18.clone | all-reduce | flops 1024 | bytes 8192
  293.7 18.3 %reduce-scatter.5.cloned.1.call-done = f32[256,512]{1,0:T(8,128)} async-done(((f32[1024,512]{1,0:T(8,128)}), f32[256,512]{1,0:T(8,128)}) %reduce-scatter.5.cloned.1.call-update) | async-done | bytes 524304 | tf_op jit(solution)/shard_map/reduce_scatter | solution.py:99
  312.0 1.9 divide_convert_fusion
  314.0 0.7 add.186
  314.7 16.2 %all-gather.5.cloned.1.call-done = bf16[1024,512]{1,0:T(8,128)(2,1)} async-done(((bf16[256,512]{1,0:T(8,128)(2,1)}), bf16[1024,512]{1,0:T(8,128)(2,1)}) %all-gather.5.cloned.1.call-update) | async-done | bytes 1048592 | tf_op jit(solution)/shard_map/all_gather | solution.py:106
  330.8 2.3 copy.100
  (64 shorter events, 3.9 us)
Async XLA Ops:
  7.2 1.6 copy-start
  27.5 7.6 %copy-start.4 = (bf16[1024,512]{1,0:T(8,128)(2,1)S(1)}, bf16[1024,512]{1,0:T(8,128)(2,1)}, u32[]{:S(2)}) copy-start(bf16[1024,512]{1,0:T(8,128)(2,1)} %param.4) | copy-start | bytes 3145732
  27.5 112.0 %all-to-all-start = ((bf16[4,8,9,16,512]{4,3,2,0,1:T(8,128)(2,1)}), bf16[4,8,9,16,512]{4,3,2,0,1:T(8,128)(2,1)}, u32[]{:S(2)}, u32[]{:S(2)}) async-start(bf16[4,8,9,16,512]{4,3,2,0,1:T(8,128)(2,1)} %copy.70), calls=%async_computation | async-start | bytes 9437184 | tf_op jit(solution)/shard_map/all_to_all | solution.py:72
  139.5 14.1 %all-to-all-start.3 = ((bf16[8,2,288]{2,1,0:T(2,128)(2,1)}), bf16[8,2,288]{2,1,0:T(2,128)(2,1)S(1)}, u32[]{:S(2)}, u32[]{:S(2)}) async-start(bf16[8,2,288]{2,1,0:T(2,128)(2,1)} %reshape.400), calls=%async_computation.3 | async-start | bytes 24576 | tf_op jit(solution)/shard_map/all_to_all | solution.py:73
  146.0 2.1 copy-start.1
  148.1 2.2 copy-start.2
  153.6 12.6 %all-to-all-start.1 = ((f32[8,1,576]{2,1,0:T(1,128)}), f32[8,1,576]{2,1,0:T(1,128)S(1)}, u32[]{:S(2)}, u32[]{:S(2)}) async-start(f32[8,1,576]{2,1,0:T(1,128)} %reshape.402), calls=%async_computation.1 | async-start | bytes 40960 | tf_op jit(solution)/shard_map/all_to_all | solution.py:81
  176.2 9.9 %all-to-all-start.2 = ((f32[8,1,576]{2,1,0:T(1,128)}), f32[8,1,576]{2,1,0:T(1,128)S(1)}, u32[]{:S(2)}, u32[]{:S(2)}) async-start(f32[8,1,576]{2,1,0:T(1,128)} %reshape.404), calls=%async_computation.2 | async-start | bytes 40960 | tf_op jit(solution)/shard_map/all_to_all | solution.py:87
  179.5 44.5 %reduce-scatter.3.cloned.1.call-start = ((), (), s32[]{:S(2)}) async-start(), calls=%async_computation.8 | async-start | bytes 2621440 | tf_op jit(solution)/shard_map/reduce_scatter | solution.py:99
  188.7 6.7 %copy-start.5 = (u32[32]{0:T(128)S(1)}, u32[32]{0:T(128)}, u32[]{:S(2)}) copy-start(u32[32]{0:T(128)} %constant.77) | copy-start | bytes 388
  195.4 47.5 %all-gather.3.cloned.1.call-start = ((), (), s32[]{:S(2)}) async-start(), calls=%async_computation.9 | async-start | bytes 1310720 | tf_op jit(solution)/shard_map/all_gather | solution.py:106
  225.9 86.2 %reduce-scatter.5.cloned.1.call-start = ((), (), s32[]{:S(2)}) async-start(), calls=%async_computation.10 | async-start | bytes 2621440 | tf_op jit(solution)/shard_map/reduce_scatter | solution.py:99
  248.6 2.2 copy-start.3
  284.3 46.5 %all-gather.5.cloned.1.call-start = ((), (), s32[]{:S(2)}) async-start(), calls=%async_computation.11 | async-start | bytes 1310720 | tf_op jit(solution)/shard_map/all_gather | solution.py:106
Sparse Core Ops, SparseCore 0:
  195.5 28.4 reduce-scatter.2
  226.1 16.6 all-gather.2
  284.5 27.5 reduce-scatter.4
  314.1 16.6 all-gather.4
where the time goes:
time: 341 us; the launch traced here: 340 us
  waiting for transfers between devices  183 us (54%)
  local copies, waits for them, and re-layouts  46.7 us (14%)
  blocking collectives  32.3 us (9%)
  other arithmetic  22.3 us (7%)
  starting transfers between devices  20.8 us (6%)
  matrix products  19.3 us (6%)
  between operations  14.8 us (4%)
    all_to_all x1, waiting for transfers between devices, on_device(): lax.all_to_all(outgoing, 'pts', split_axis=1, concat_axis=1, tiled=True)  103 us
    reduce_scatter x2, waiting for transfers between devices, on_device(): lax.psum_scatter(weighted, 'cent', scatter_dimension=0, tiled=True)  36.3 us
    all_gather x2, waiting for transfers between devices, on_device(): current = lax.all_gather(renewed, 'cent', axis=0, tiled=True)  33.1 us
    gather x1, local copies, waits for them, and re-layouts, on_device(): grouped[home_block]  13.3 us
    dot_general x2, matrix products, on_device(): jnp.einsum('lsm,lsd->lmd', rounded, flat_rows, preferred_element_type=jnp...  13.3 us
    unnamed x28, local copies, waits for them, and re-layouts  11.9 us
    all_to_all x1, blocking collectives, on_device(): lax.all_to_all(partial_value, 'pts', split_axis=1, concat_axis=1, tiled=T...  11.9 us
    unnamed x2, blocking collectives  11.4 us
  transfers between devices with their start and end apart: 8, of which 7 were waited for; matrix products, arithmetic and copies ran while one was open for 6% of the time, Pallas kernels for 0%

commit v1 on v0

--- a/solution.py
+++ b/solution.py
@@ -1,8 +1,11 @@
+import functools
 import math
 
 import jax
 import jax.numpy as jnp
 from jax import lax
+from jax.experimental import pallas as pl
+from jax.experimental.pallas import tpu as pltpu
 from jax.sharding import PartitionSpec as P
 
 CB = 256
@@ -32,7 +35,7 @@
     return scoring
 
 
-def on_device(points, centroids, candidates):
+def exchange_points(points, centroids, candidates):
     feature_width = points.shape[1]
     inverse_root = 1.0 / math.sqrt(feature_width)
     owners = lax.axis_size("pts")
@@ -107,6 +110,143 @@
     return (current, point_lse.reshape(-1))
 
 
+def em_kernel(
+    blocks, capacity, inverse_root, source, points, table, sums, masses, lse_out,
+    rows_held, score_held, partial_held, lse_held,
+):
+    width = table.shape[1]
+    group = capacity * PB
+    entries = partial_held.shape[0] - 1
+    point_blocks = entries // 2
+    ones = jnp.ones((8, width), jnp.bfloat16)
+    across = (((1,), (1,)), ((), ()))
+
+    @pl.loop(0, blocks)
+    def _(b):
+        for c in range(capacity):
+            home = jnp.maximum(source[b * capacity + c], 0) // 2
+            rows_held[b, pl.ds(c * PB, PB), :] = points[home]
+        centre = table[pl.ds(pl.multiple_of(b * CB, CB), CB), :]
+        wide = centre.astype(jnp.float32)
+        square = wide * wide
+        high = square.astype(jnp.bfloat16)
+        low = (square - high.astype(jnp.float32)).astype(jnp.bfloat16)
+        norms = lax.dot_general(ones, high, across, preferred_element_type=jnp.float32)
+        norms += lax.dot_general(ones, low, across, preferred_element_type=jnp.float32)
+        products = lax.dot_general(
+            rows_held[b], centre, across, preferred_element_type=jnp.float32
+        )
+        scores = inverse_root * (2.0 * products - norms[0:1, :])
+        highest = jnp.max(scores, axis=1, keepdims=True)
+        partial = highest + jnp.log(jnp.sum(jnp.exp(scores - highest), axis=1, keepdims=True))
+        partial = jnp.broadcast_to(partial, (group, 128))
+        score_held[b] = scores
+        for c in range(capacity):
+            entry = source[b * capacity + c]
+            partial_held[jnp.where(entry < 0, entries, entry)] = partial[c * PB : (c + 1) * PB]
+
+    @pl.loop(0, point_blocks // 8)
+    def _(i):
+        for j in range(8):
+            g = i * 8 + j
+            first, second = partial_held[2 * g], partial_held[2 * g + 1]
+            highest = jnp.maximum(first, second)
+            value = highest + jnp.log(jnp.exp(first - highest) + jnp.exp(second - highest))
+            lse_held[g] = value
+            lse_out[g] = value
+
+    lse_held[point_blocks] = jnp.full((PB, 128), 1e30, jnp.float32)
+
+    @pl.loop(0, blocks)
+    def _(b):
+        taken = []
+        for c in range(capacity):
+            entry = source[b * capacity + c]
+            taken.append(lse_held[jnp.where(entry < 0, point_blocks, entry // 2)])
+        lse = jnp.concatenate(taken, axis=0)
+        lse = jnp.concatenate([lse] * (CB // 128), axis=1)
+        weights = jnp.exp(score_held[b] - lse)
+        masses[b] = jnp.sum(weights, axis=0, keepdims=True)
+        total = lax.dot_general(
+            weights.astype(jnp.bfloat16), rows_held[b], (((0,), (0,)), ((), ())),
+            preferred_element_type=jnp.float32,
+        )
+        sums[pl.ds(pl.multiple_of(b * CB, CB), CB), :] = total.astype(sums.dtype)
+
+
+def exchange_centroids(points, centroids, candidates):
+    width = points.shape[1]
+    axes = ("pts", "cent")
+    devices = lax.axis_size("pts") * lax.axis_size("cent")
+    point_blocks = candidates.shape[0]
+    total_rows = centroids.shape[0] * lax.axis_size("pts")
+    blocks = total_rows // CB
+    capacity = max(2, 2 * point_blocks // blocks + 1)
+    entries = 2 * point_blocks
+    picked = candidates.reshape(-1)
+    labels = jnp.arange(blocks, dtype=jnp.int32)
+    member = (picked[:, None] == labels[None, :]).astype(jnp.bfloat16)
+    entry_index = jnp.arange(entries, dtype=jnp.int32)
+    earlier = (entry_index[None, :] < entry_index[:, None]).astype(jnp.bfloat16)
+    prior_hits = jnp.dot(earlier, member, preferred_element_type=jnp.float32)
+    arrival = jnp.sum(prior_hits * member.astype(jnp.float32), axis=1).astype(jnp.int32)
+    position = picked * capacity + arrival
+    places = jnp.arange(blocks * capacity, dtype=jnp.int32)
+    source = (
+        jnp.sum(
+            jnp.where(position[:, None] == places[None, :], entry_index[:, None] + 1, 0), axis=0
+        )
+        - 1
+    )
+    group = capacity * PB
+    vmem = pl.BlockSpec(memory_space=pltpu.VMEM)
+    round_call = pl.pallas_call(
+        functools.partial(em_kernel, blocks, capacity, 1.0 / math.sqrt(width)),
+        out_shape=(
+            jax.ShapeDtypeStruct((total_rows, width), jnp.bfloat16),
+            jax.ShapeDtypeStruct((blocks, 1, CB), jnp.float32),
+            jax.ShapeDtypeStruct((point_blocks, PB, 128), jnp.float32),
+        ),
+        in_specs=[pl.BlockSpec(memory_space=pltpu.SMEM), vmem, vmem],
+        out_specs=(vmem, vmem, vmem),
+        scratch_shapes=[
+            pltpu.VMEM((blocks, group, width), jnp.bfloat16),
+            pltpu.VMEM((blocks, group, CB), jnp.float32),
+            pltpu.VMEM((entries + 1, PB, 128), jnp.float32),
+            pltpu.VMEM((point_blocks + 1, PB, 128), jnp.float32),
+        ],
+        compiler_params=pltpu.CompilerParams(vmem_limit_bytes=50 << 20),
+    )
+    grouped = points.reshape(point_blocks, PB, width)
+    share_rows = total_rows // devices
+    share = lax.dynamic_slice_in_dim(
+        centroids, lax.axis_index("cent") * share_rows, share_rows, 0
+    )
+    for iteration in range(ITERS):
+        table = lax.all_gather(share, axes, axis=0, tiled=True)
+        sums, masses, lse = round_call(source, grouped, table)
+        share_sums = lax.psum_scatter(sums, axes, scatter_dimension=0, tiled=True)
+        share_mass = lax.psum_scatter(
+            masses.reshape(total_rows), axes, scatter_dimension=0, tiled=True
+        )
+        share = (share_sums.astype(jnp.float32) + share.astype(jnp.float32)) / (
+            share_mass[:, None] + 1.0
+        )
+        share = share.astype(jnp.bfloat16)
+    return (lax.all_gather(share, "cent", axis=0, tiled=True), lse[:, :, 0].reshape(-1))
+
+
+def on_device(points, centroids, candidates):
+    width = points.shape[1]
+    table_size = centroids.shape[0] * lax.axis_size("pts") * width
+    blocks = table_size // width // CB
+    slots = blocks * max(2, 2 * candidates.shape[0] // blocks + 1)
+    held = 4 * table_size + 2 * points.size + slots * PB * (2 * width + 4 * CB)
+    if held <= 40 << 20 and candidates.shape[0] % 8 == 0:
+        return exchange_centroids(points, centroids, candidates)
+    return exchange_points(points, centroids, candidates)
+
+
 def solution(mesh):
     return jax.shard_map(
         on_device,

time: 341 us -> 560 us (1.64)
  waiting for transfers between devices: 183 us -> 383 us
  Pallas kernels: 0 us -> 69.3 us
  blocking collectives: 32.3 us -> 82.2 us
  local copies, waits for them, and re-layouts: 46.7 us -> 7.49 us
  starting transfers between devices: 20.8 us -> 0.21 us
  matrix products: 19.3 us -> 0.21 us
  other arithmetic: 22.3 us -> 3.93 us
    reduce_scatter x2, waiting for transfers between devices: 36.3 us -> 215 us  [exchange_centroids(): share_sums = lax.psum_scatter(sums, axes, scatter_dimension=0, tiled=True)]
    all_gather x2 -> x3, waiting for transfers between devices: 33.1 us -> 167 us  [the longest x2 155 us: exchange_centroids(): table = lax.all_gather(share, axes, axis=0, tiled=True)]
    all_to_all x4 -> x0, waiting for transfers between devices: 114 us -> none  [the longest x1 103 us: on_device(): lax.all_to_all(outgoing, 'pts', split_axis=1, concat_axis=1, tiled=True)]
    unnamed x2, blocking collectives: 11.4 us -> 82.2 us
    pallas_call x0 -> x2, Pallas kernels: none -> 69.3 us  [exchange_centroids(): sums, masses, lse = round_call(source, grouped, table)]
    all_to_all x2 -> x0, blocking collectives: 20.9 us -> none  [the longest x1 11.9 us: on_device(): lax.all_to_all(partial_value, 'pts', split_axis=1, concat_axis=1, tiled=T...]
    all_to_all x4 -> x0, starting transfers between devices: 20.4 us -> none  [the longest x1 7.44 us: on_device(): lax.all_to_all(outgoing, 'pts', split_axis=1, concat_axis=1, tiled=True)]
    dot_general x5 -> x1, matrix products: 19.3 us -> 0.21 us  [exchange_centroids(): prior_hits = jnp.dot(earlier, member, preferred_element_type=jnp.float32)]
  transfers between devices with their start and end apart: 8 -> 5, of which waited for: 7 -> 5; matrix products, arithmetic and copies ran while one was open for 6% -> 0% of each run, Pallas kernels for 0% -> 0%
where the time goes in v1:
time: 560 us
  waiting for transfers between devices  383 us (68%)
  blocking collectives  82.2 us (15%)
  Pallas kernels  69.3 us (12%)
  between operations  13.8 us (2%)
  local copies, waits for them, and re-layouts  7.49 us (1%)
    reduce_scatter x2, waiting for transfers between devices, exchange_centroids(): share_sums = lax.psum_scatter(sums, axes, scatter_dimension=0, tiled=True)  215 us
    all_gather x2, waiting for transfers between devices, exchange_centroids(): table = lax.all_gather(share, axes, axis=0, tiled=True)  155 us
    unnamed x2, blocking collectives  82.2 us
    pallas_call x2, Pallas kernels, exchange_centroids(): sums, masses, lse = round_call(source, grouped, table)  69.3 us
    all_gather x1, waiting for transfers between devices, exchange_centroids(): lax.all_gather(share, 'cent', axis=0, tiled=True)  11.8 us
  transfers between devices with their start and end apart: 5, of which 5 were waited for; matrix products, arithmetic and copies ran while one was open for 0% of the time, Pallas kernels for 0%

profile of v1, /device:TPU:0, one launch (start us, length us, event | category | flops | bytes accessed | tf_op | source)
XLA Modules:
  0.0 559.7 jit_solution(8692979444628530137)
XLA Ops:
  7.2 0.0 all-gather.4.cloned.1.call-start
  7.2 1.7 constant_dynamic-slice_fusion
  8.9 0.0 all-gather.4.cloned.1.call-update
  8.9 0.0 reduce-scatter.3.cloned.1.call-start
  9.0 0.8 copy.7
  9.8 0.1 reshape.35
  9.9 0.2 fusion
  10.1 0.1 select_reduce_fusion
  10.3 80.9 %all-gather.4.cloned.1.call-done.table = bf16[8192,512]{1,0:T(8,128)(2,1)} async-done(((bf16[256,512]{1,0:T(8,128)(2,1)}), bf16[8192,512]{1,0:T(8,128)(2,1)}) %all-gather.4.cloned.1.call-update) | async-done | bytes 8388624 | tf_op jit(solution)/shard_map/all_gather | solution.py:226
  91.2 0.0 copy-start
  91.2 1.6 copy-done
  92.8 0.0 copy-start.1
  92.8 34.8 %shard_map.50 = (bf16[8192,512]{1,0:T(8,128)(2,1)}, f32[32,1,256]{2,1,0:T(1,128)S(1)}, f32[128,16,128]{2,1,0:T(8,128)}) custom-call(s32[288]{0:T(512)S(1)} %broadcast_add_fusion.source, bf16[128,16,512]{2,1,0:T(8,128)(2,1)S(1)} %bitcast.3, bf16[8192,512]{1,0:T(8,128)(2,1)} %all-gather.4.cloned.1.call-done.table), custom_call_target="tpu_custom_call" | custom-call | tf_op jit(solution)/shard_map/pallas_call | solution.py:227
  127.6 0.0 reduce-scatter.3.cloned.1.call-update
  127.6 0.0 all-gather.6.cloned.1.call-start
  127.7 41.2 %all-reduce = f32[8192]{0:T(1024)S(1)} all-reduce(f32[8192]{0:T(1024)S(1)} %bitcast.5), channel_id=3, replica_groups=mesh['pts'=8,'cent'=4] {'pts','cent'}, use_global_device_ids=true, to_apply=%region_3.4.clone | all-reduce | flops 8192 | bytes 65536
  168.8 0.1 dynamic-slice_add_fusion.1
  168.9 107.5 %reduce-scatter.3.cloned.1.call-done = bf16[256,512]{1,0:T(8,128)(2,1)} async-done(((bf16[8192,512]{1,0:T(8,128)(2,1)}), bf16[256,512]{1,0:T(8,128)(2,1)}) %reduce-scatter.3.cloned.1.call-update) | async-done | bytes 262160 | tf_op jit(solution)/shard_map/reduce_scatter | solution.py:228
  276.4 1.8 divide_convert_fusion.1
  278.2 0.0 all-gather.6.cloned.1.call-update
  278.3 0.0 copy-start.2
  278.3 0.0 reduce-scatter.5.cloned.1.call-start
  278.3 74.5 %all-gather.6.cloned.1.call-done.table = bf16[8192,512]{1,0:T(8,128)(2,1)} async-done(((bf16[256,512]{1,0:T(8,128)(2,1)}), bf16[8192,512]{1,0:T(8,128)(2,1)}) %all-gather.6.cloned.1.call-update) | async-done | bytes 8388624 | tf_op jit(solution)/shard_map/all_gather | solution.py:226
  352.8 0.0 copy-done.1
  352.8 34.5 %shard_map.51 = (bf16[8192,512]{1,0:T(8,128)(2,1)}, f32[32,1,256]{2,1,0:T(1,128)S(1)}, f32[128,16,128]{2,1,0:T(8,128)S(1)}) custom-call(s32[288]{0:T(512)S(1)} %broadcast_add_fusion.source, bf16[128,16,512]{2,1,0:T(8,128)(2,1)S(1)} %bitcast.4, bf16[8192,512]{1,0:T(8,128)(2,1)} %all-gather.6.cloned.1.call-done.table), custom_call_target="tpu_custom_call" | custom-call | tf_op jit(solution)/shard_map/pallas_call | solution.py:227
  387.3 0.0 reduce-scatter.5.cloned.1.call-update
  387.3 0.0 all-gather.8.cloned.1.call-start
  387.4 41.0 %all-reduce.1 = f32[8192]{0:T(1024)S(1)} all-reduce(f32[8192]{0:T(1024)S(1)} %bitcast.6), channel_id=5, replica_groups=mesh['pts'=8,'cent'=4] {'pts','cent'}, use_global_device_ids=true, to_apply=%region_5.6.clone | all-reduce | flops 8192 | bytes 65536
  428.4 0.1 dynamic-slice_add_fusion
  428.5 107.8 %reduce-scatter.5.cloned.1.call-done = bf16[256,512]{1,0:T(8,128)(2,1)} async-done(((bf16[8192,512]{1,0:T(8,128)(2,1)}), bf16[256,512]{1,0:T(8,128)(2,1)}) %reduce-scatter.5.cloned.1.call-update) | async-done | bytes 262160 | tf_op jit(solution)/shard_map/reduce_scatter | solution.py:228
  536.3 0.0 copy-done.2
  536.3 1.8 divide_convert_fusion
  538.1 0.0 all-gather.8.cloned.1.call-update
  538.1 0.3 slice_reduce_fusion
  538.5 0.7 reshape_squeeze.3
  539.1 11.8 %all-gather.8.cloned.1.call-done = bf16[1024,512]{1,0:T(8,128)(2,1)} async-done(((bf16[256,512]{1,0:T(8,128)(2,1)}), bf16[1024,512]{1,0:T(8,128)(2,1)}) %all-gather.8.cloned.1.call-update) | async-done | bytes 1048592 | tf_op jit(solution)/shard_map/all_gather | solution.py:236
  550.9 2.3 copy.9
  (2 shorter events, 0.0 us)
Async XLA Ops:
  7.2 84.0 %all-gather.4.cloned.1.call-start = ((), (), s32[]{:S(2)}) async-start(), calls=%async_computation.2 | async-start | bytes 8650752 | tf_op jit(solution)/shard_map/all_gather | solution.py:226
  8.9 267.5 %reduce-scatter.3.cloned.1.call-start = ((), (), s32[]{:S(2)}) async-start(), calls=%async_computation.3 | async-start | bytes 8650752 | tf_op jit(solution)/shard_map/reduce_scatter | solution.py:228
  91.2 1.6 copy-start
  92.8 260.0 %copy-start.1 = (bf16[2048,512]{1,0:T(8,128)(2,1)S(1)}, bf16[2048,512]{1,0:T(8,128)(2,1)}, u32[]{:S(2)}) copy-start(bf16[2048,512]{1,0:T(8,128)(2,1)} %param.3) | copy-start | bytes 6291460
  127.6 225.2 %all-gather.6.cloned.1.call-start = ((), (), s32[]{:S(2)}) async-start(), calls=%async_computation.4 | async-start | bytes 8650752 | tf_op jit(solution)/shard_map/all_gather | solution.py:226
  278.3 258.0 %copy-start.2 = (bf16[256,512]{1,0:T(8,128)(2,1)S(1)}, bf16[256,512]{1,0:T(8,128)(2,1)}, u32[]{:S(2)}) copy-start(bf16[256,512]{1,0:T(8,128)(2,1)} %divide_convert_fusion.1) | copy-start | bytes 786436
  278.3 258.0 %reduce-scatter.5.cloned.1.call-start = ((), (), s32[]{:S(2)}) async-start(), calls=%async_computation.5 | async-start | bytes 8650752 | tf_op jit(solution)/shard_map/reduce_scatter | solution.py:228
  387.3 163.5 %all-gather.8.cloned.1.call-start = ((), (), s32[]{:S(2)}) async-start(), calls=%async_computation.6 | async-start | bytes 1310720 | tf_op jit(solution)/shard_map/all_gather | solution.py:236
Sparse Core Ops, SparseCore 0:
  11.4 79.7 all-gather.3
  127.7 148.6 reduce-scatter.2
  279.8 72.8 all-gather.5
  387.5 148.7 reduce-scatter.4
  538.3 12.5 all-gather.7

commit v2 on v0

--- a/solution.py
+++ b/solution.py
@@ -3,6 +3,8 @@
 import jax
 import jax.numpy as jnp
 from jax import lax
+from jax.experimental import pallas as pl
+from jax.experimental.pallas import tpu as pltpu
 from jax.sharding import PartitionSpec as P
 
 CB = 256
@@ -16,10 +18,27 @@
     return jnp.squeeze(highest, reduce_axis) + jnp.log(summed)
 
 
+def pick_kernel(home_block, grouped, outgoing):
+    @pl.loop(0, outgoing.shape[0])
+    def _(slot):
+        outgoing[slot] = grouped[home_block[slot]]
+
+
+def pick_blocks(home_block, grouped):
+    vmem = pl.BlockSpec(memory_space=pltpu.VMEM)
+    return pl.pallas_call(
+        pick_kernel,
+        out_shape=jax.ShapeDtypeStruct(home_block.shape + grouped.shape[1:], grouped.dtype),
+        in_specs=[pl.BlockSpec(memory_space=pltpu.SMEM), vmem],
+        out_specs=vmem,
+        compiler_params=pltpu.CompilerParams(vmem_limit_bytes=32 << 20),
+    )(home_block, grouped)
+
+
 def make_scoring(centre_table, centre_norms, inverse_root):
 
     def scoring(package):
-        slot_rows, slot_flags = package
+        slot_rows = package
         leading = slot_rows.shape[0]
         flat_rows = slot_rows.reshape(leading, -1, slot_rows.shape[-1])
         products = jnp.einsum(
@@ -27,7 +46,7 @@
         )
         scores = inverse_root * (2.0 * products - centre_norms[:, None, :])
         scores = scores.reshape(slot_rows.shape[:-1] + (centre_table.shape[1],))
-        return (slot_rows, slot_flags, scores, stable_lse(scores, scores.ndim - 1))
+        return (scores, stable_lse(scores, scores.ndim - 1))
 
     return scoring
 
@@ -64,28 +83,23 @@
     )
     filled = source >= 0
     home_block = jnp.maximum(source, 0) // 2
-    outgoing = jnp.where(filled[:, None, None], grouped[home_block], jnp.zeros((), jnp.bfloat16))
+    outgoing = pick_blocks(home_block, grouped)
     outgoing = outgoing.reshape(slot_shape + (PB, feature_width))
-    slot_marks = jnp.broadcast_to(filled[:, None], (slot_count, PB)).astype(jnp.bfloat16)
-    slot_marks = slot_marks.reshape(slot_shape + (PB,))
     point_lse = jnp.zeros((point_blocks, PB), jnp.float32)
     arrived = lax.all_to_all(outgoing, "pts", split_axis=1, concat_axis=1, tiled=True)
-    arrived_marks = lax.all_to_all(slot_marks, "pts", split_axis=1, concat_axis=1, tiled=True)
     for iteration in range(ITERS):
         centre_table = current.reshape(-1, CB, feature_width)
         centre_norms = jnp.sum(jnp.square(centre_table.astype(jnp.float32)), axis=2)
         scoring = make_scoring(centre_table, centre_norms, inverse_root)
-        arrived, arrived_marks, scores, partial_value = scoring(
-            (arrived, arrived_marks)
-        )
+        scores, partial_value = scoring(arrived)
         returned = lax.all_to_all(partial_value, "pts", split_axis=1, concat_axis=1, tiled=True)
         per_entry = returned.reshape(slot_count, PB)[position]
         paired = per_entry.reshape(point_blocks, 2, PB)
         point_lse = stable_lse(paired, 1)
-        outward = jnp.where(filled[:, None], point_lse[home_block], jnp.zeros((), jnp.float32))
+        outward = jnp.where(filled[:, None], point_lse[home_block], jnp.float32(1e30))
         outward = outward.reshape(slot_shape + (PB,))
         inward = lax.all_to_all(outward, "pts", split_axis=1, concat_axis=1, tiled=True)
-        weights = jnp.exp(scores - inward[..., None]) * arrived_marks.astype(jnp.float32)[..., None]
+        weights = jnp.exp(scores - inward[..., None])
         leading = weights.shape[0]
         flat_weights = weights.reshape(leading, -1, CB)
         masses = jnp.sum(flat_weights, axis=1).reshape(leading * CB)
@@ -94,7 +108,7 @@
         weighted = jnp.einsum(
             "lsm,lsd->lmd", rounded, flat_rows, preferred_element_type=jnp.float32
         )
-        weighted = weighted.reshape(leading * CB, feature_width)
+        weighted = weighted.astype(jnp.bfloat16).reshape(leading * CB, feature_width)
         share_sums, share_mass = (
             lax.psum_scatter(weighted, "cent", scatter_dimension=0, tiled=True),
             lax.psum_scatter(masses, "cent", scatter_dimension=0, tiled=True),
@@ -102,7 +116,7 @@
         share_rows = share_sums.shape[0]
         first_row = lax.axis_index("cent") * share_rows
         previous = lax.dynamic_slice_in_dim(current, first_row, share_rows, 0).astype(jnp.float32)
-        renewed = ((share_sums + previous) / (share_mass[:, None] + 1.0)).astype(jnp.bfloat16)
+        renewed = ((share_sums.astype(jnp.float32) + previous) / (share_mass[:, None] + 1.0)).astype(jnp.bfloat16)
         current = lax.all_gather(renewed, "cent", axis=0, tiled=True)
     return (current, point_lse.reshape(-1))
 

time: 341 us -> 299 us (0.88)
  local copies, waits for them, and re-layouts: 46.7 us -> 24.6 us
  waiting for transfers between devices: 183 us -> 168 us
  starting transfers between devices: 20.8 us -> 11.4 us
  blocking collectives: 32.3 us -> 41.3 us
  other arithmetic: 22.3 us -> 17.2 us
    gather x1 -> x0, local copies, waits for them, and re-layouts: 13.3 us -> none  [on_device(): grouped[home_block]]
    reduce_scatter x2, waiting for transfers between devices: 36.3 us -> 24.1 us  [on_device(): lax.psum_scatter(weighted, 'cent', scatter_dimension=0, tiled=True)]
    all_to_all x1 -> x2, blocking collectives: 8.97 us -> 17.9 us  [on_device(): lax.all_to_all(outward, 'pts', split_axis=1, concat_axis=1, tiled=True)]
    all_to_all x2 -> x0, starting transfers between devices: 6.97 us -> none  [the longest x1 3.64 us: on_device(): lax.all_to_all(slot_marks, 'pts', split_axis=1, concat_axis=1, tiled=True)]
    all_to_all x2 -> x0, waiting for transfers between devices: 4.48 us -> none  [the longest x1 4.47 us: on_device(): lax.all_to_all(outward, 'pts', split_axis=1, concat_axis=1, tiled=True)]
    select_n x4, other arithmetic: 4.36 us -> 0.09 us  [the longest x2 0.06 us: on_device(): jnp.where(filled[:, None], point_lse[home_block], jnp.float32(1e+30))]
    select_n x3 -> x2, local copies, waits for them, and re-layouts: 4.21 us -> 0.58 us  [on_device(): jnp.where(filled[:, None], point_lse[home_block], jnp.float32(1e+30))]
    unnamed x28 -> x25, local copies, waits for them, and re-layouts: 11.9 us -> 11.8 us
  transfers between devices with their start and end apart: 8 -> 6, of which waited for: 7 -> 6; matrix products, arithmetic and copies ran while one was open for 6% -> 3% of each run, Pallas kernels for 0% -> 0%
where the time goes in v2:
time: 299 us; the launch traced here: 298 us
  waiting for transfers between devices  168 us (56%)
  blocking collectives  41.3 us (14%)
  local copies, waits for them, and re-layouts  24.6 us (8%)
  matrix products  18.7 us (6%)
  other arithmetic  17.2 us (6%)
  between operations  14.9 us (5%)
  starting transfers between devices  11.4 us (4%)
    all_to_all x1, waiting for transfers between devices, on_device(): lax.all_to_all(outgoing, 'pts', split_axis=1, concat_axis=1, tiled=True)  104 us
    all_gather x2, waiting for transfers between devices, on_device(): current = lax.all_gather(renewed, 'cent', axis=0, tiled=True)  33 us
    reduce_scatter x2, waiting for transfers between devices, on_device(): lax.psum_scatter(weighted, 'cent', scatter_dimension=0, tiled=True)  24.1 us
    all_to_all x2, blocking collectives, on_device(): lax.all_to_all(outward, 'pts', split_axis=1, concat_axis=1, tiled=True)  17.9 us
    dot_general x2, matrix products, on_device(): jnp.einsum('lsm,lsd->lmd', rounded, flat_rows, preferred_element_type=jnp...  12.6 us
    all_to_all x1, blocking collectives, on_device(): lax.all_to_all(partial_value, 'pts', split_axis=1, concat_axis=1, tiled=T...  11.9 us
    unnamed x25, local copies, waits for them, and re-layouts  11.8 us
    unnamed x2, blocking collectives  11.4 us
  transfers between devices with their start and end apart: 6, of which 6 were waited for; matrix products, arithmetic and copies ran while one was open for 3% of the time, Pallas kernels for 0%

profile of v2, /device:TPU:0, one launch (start us, length us, event | category | flops | bytes accessed | tf_op | source)
XLA Modules:
  0.0 297.9 jit_solution(2659774495322360474)
XLA Ops:
  7.2 0.8 copy.31
  7.9 0.1 reshape.319
  8.1 0.2 fusion.20
  8.3 0.1 select_reduce_fusion
  8.5 1.6 copy-done
  10.1 2.2 shard_map.50
  12.3 2.7 copy.32
  15.0 7.4 %all-to-all-start = ((bf16[4,8,9,16,512]{4,3,2,0,1:T(8,128)(2,1)}), bf16[4,8,9,16,512]{4,3,2,0,1:T(8,128)(2,1)}, u32[]{:S(2)}, u32[]{:S(2)}) async-start(bf16[4,8,9,16,512]{4,3,2,0,1:T(8,128)(2,1)} %copy.32), calls=%async_computation | async-start | bytes 9437184 | tf_op jit(solution)/shard_map/all_to_all | solution.py:89
  22.4 0.1 reshape.325
  22.6 0.3 multiply_reduce_fusion.1
  23.0 104.0 %all-to-all-done = bf16[4,8,9,16,512]{4,3,2,0,1:T(8,128)(2,1)} async-done(((bf16[4,8,9,16,512]{4,3,2,0,1:T(8,128)(2,1)}), bf16[4,8,9,16,512]{4,3,2,0,1:T(8,128)(2,1)}, u32[]{:S(2)}, u32[]{:S(2)}) %all-to-all-start) | async-done | bytes 4718624 | tf_op jit(solution)/shard_map/all_to_all | solution.py:89
  127.0 2.8 copy.33
  129.8 1.7 fusion.30
  131.5 0.4 copy-done.1
  131.9 2.2 copy-done.2
  134.1 0.6 exponential_reduce_fusion.1
  135.0 0.8 reshape.375
  135.8 3.6 %all-to-all-start.1 = ((f32[8,1,576]{2,1,0:T(1,128)}), f32[8,1,576]{2,1,0:T(1,128)S(1)}, u32[]{:S(2)}, u32[]{:S(2)}) async-start(f32[8,1,576]{2,1,0:T(1,128)} %reshape.375), calls=%async_computation.1 | async-start | bytes 40960 | tf_op jit(solution)/shard_map/all_to_all | solution.py:95
  139.6 6.4 %all-to-all-done.1 = f32[8,1,576]{2,1,0:T(1,128)S(1)} async-done(((f32[8,1,576]{2,1,0:T(1,128)}), f32[8,1,576]{2,1,0:T(1,128)S(1)}, u32[]{:S(2)}, u32[]{:S(2)}) %all-to-all-start.1) | async-done | bytes 18464 | tf_op jit(solution)/shard_map/all_to_all | solution.py:95
  146.0 0.5 broadcast.347
  146.5 0.7 reduce.8
  147.2 0.1 reshape.376
  147.4 0.7 gather_fusion
  148.2 0.2 reduce_max.37
  148.3 0.2 exponential_reduce_fusion.3
  148.6 1.1 gather_fusion.1
  149.7 0.3 gather.18
  150.1 0.3 copy.39
  150.4 0.1 reshape.377
  150.5 9.0 %all_to_all.25 = f32[8,1,576]{2,1,0:T(1,128)S(1)} all-to-all(f32[8,1,576]{2,1,0:T(1,128)S(1)} %reshape.377), channel_id=1, replica_groups=mesh['pts'=8,'cent'=4] {'pts'}, dimensions={0} | all-to-all | bytes 36864 | tf_op jit(solution)/shard_map/all_to_all | solution.py:101
  159.5 0.7 reduce.9
  160.2 0.1 reshape.378
  160.5 6.3 %fusion.14 = bf16[4,256,512]{2,1,0:T(8,128)(2,1)} fusion(bf16[4,1152,512]{2,1,0:T(8,128)(2,1)} %bitcast.41, f32[4,1152,256]{1,2,0:T(8,128)} %copy-done.2, f32[4,1152]{1,0:T(4,128)S(1)} %sub.108), kind=kOutput, calls=%fused_computation.24 | convolution fusion | flops 1210843136 | bytes 10504192 | tf_op jit(solution)/shard_map/lsm,lsd->lmd/dot_general | solution.py:108
  166.9 0.7 dynamic-slice
  168.2 3.2 %fusion.4 = f32[4,256]{1,0:T(4,128)S(1)} fusion(f32[4,1152,256]{1,2,0:T(8,128)} %copy-done.2, f32[4,1152]{1,0:T(4,128)S(1)} %sub.108), kind=kLoop, calls=%fused_computation.14 | loop fusion | flops 2358272 | bytes 4741120 | tf_op jit(solution)/shard_map/reduce_sum | solution.py:105
  171.4 5.7 %all-reduce = f32[1024]{0:T(1024)S(1)} all-reduce(f32[1024]{0:T(1024)S(1)} %bitcast.62), channel_id=3, replica_groups=mesh['pts'=8,'cent'=4] {'cent'}, use_global_device_ids=true, to_apply=%region_9.10.clone | all-reduce | flops 1024 | bytes 8192
  177.2 11.9 %reduce-scatter.3.cloned.1.call-done = bf16[256,512]{1,0:T(8,128)(2,1)} async-done(((bf16[1024,512]{1,0:T(8,128)(2,1)}), bf16[256,512]{1,0:T(8,128)(2,1)}) %reduce-scatter.3.cloned.1.call-update) | async-done | bytes 262160 | tf_op jit(solution)/shard_map/reduce_scatter | solution.py:113
  189.1 1.8 divide_convert_fusion.1
  190.8 0.2 reduce-scatter.5.cloned.1.call-start
  191.1 16.9 %all-gather.3.cloned.1.call-done = bf16[1024,512]{1,0:T(8,128)(2,1)} async-done(((bf16[256,512]{1,0:T(8,128)(2,1)}), bf16[1024,512]{1,0:T(8,128)(2,1)}) %all-gather.3.cloned.1.call-update) | async-done | bytes 1048592 | tf_op jit(solution)/shard_map/all_gather | solution.py:120
  207.9 1.5 multiply_reduce_fusion
  209.4 4.2 %fusion.31 = (f32[4,1152]{1,0:T(4,128)S(1)}, f32[4,1152,256]{1,2,0:T(8,128)S(1)}) fusion(f32[4,256]{1,0:T(4,128)S(1)} %sub.111, bf16[4,1152,512]{2,1,0:T(8,128)(2,1)} %bitcast.42, bf16[4,256,512]{2,1,0:T(8,128)(2,1)} %bitcast.47), kind=kOutput, calls=%fused_computation.75 | convolution fusion | flops 1212673536 | bytes 10508288 | tf_op jit(solution)/shard_map/lsd,lmd->lsm/dot_general | solution.py:44
  213.7 2.2 copy-done.3
  215.9 0.6 exponential_reduce_fusion
  216.8 0.1 reshape.379
  216.9 11.9 %all_to_all.26 = f32[8,1,576]{2,1,0:T(1,128)S(1)} all-to-all(f32[8,1,576]{2,1,0:T(1,128)S(1)} %reshape.379), channel_id=1, replica_groups=mesh['pts'=8,'cent'=4] {'pts'}, dimensions={0} | all-to-all | bytes 36864 | tf_op jit(solution)/shard_map/all_to_all | solution.py:95
  228.8 0.7 reduce.10
  229.7 0.7 gather_fusion.2
  230.5 0.2 reduce_max.39
  230.6 0.2 exponential_reduce_fusion.2
  230.9 1.1 gather_fusion.3
  232.0 0.3 gather.21
  232.4 0.3 copy.45
  232.7 0.1 reshape.381
  232.8 9.0 %all_to_all.27 = f32[8,1,576]{2,1,0:T(1,128)S(1)} all-to-all(f32[8,1,576]{2,1,0:T(1,128)S(1)} %reshape.381), channel_id=1, replica_groups=mesh['pts'=8,'cent'=4] {'pts'}, dimensions={0} | all-to-all | bytes 36864 | tf_op jit(solution)/shard_map/all_to_all | solution.py:101
  241.8 0.7 reduce.11
  242.8 6.3 %fusion.17 = bf16[4,256,512]{2,1,0:T(8,128)(2,1)} fusion(bf16[4,1152,512]{2,1,0:T(8,128)(2,1)} %bitcast.43, f32[4,1152,256]{1,2,0:T(8,128)} %copy-done.3, f32[4,1152]{1,0:T(4,128)S(1)} %sub.118), kind=kOutput, calls=%fused_computation.25 | convolution fusion | flops 1210843136 | bytes 10504192 | tf_op jit(solution)/shard_map/lsm,lsd->lmd/dot_general | solution.py:108
  249.1 3.2 %fusion.6 = f32[4,256]{1,0:T(4,128)S(1)} fusion(f32[4,1152,256]{1,2,0:T(8,128)} %copy-done.3, f32[4,1152]{1,0:T(4,128)S(1)} %sub.118), kind=kLoop, calls=%fused_computation.16 | loop fusion | flops 2358272 | bytes 4741120 | tf_op jit(solution)/shard_map/reduce_sum | solution.py:105
  252.3 5.8 %all-reduce.1 = f32[1024]{0:T(1024)S(1)} all-reduce(f32[1024]{0:T(1024)S(1)} %bitcast.63), channel_id=5, replica_groups=mesh['pts'=8,'cent'=4] {'cent'}, use_global_device_ids=true, to_apply=%region_17.18.clone | all-reduce | flops 1024 | bytes 8192
  258.2 12.2 %reduce-scatter.5.cloned.1.call-done = bf16[256,512]{1,0:T(8,128)(2,1)} async-done(((bf16[1024,512]{1,0:T(8,128)(2,1)}), bf16[256,512]{1,0:T(8,128)(2,1)}) %reduce-scatter.5.cloned.1.call-update) | async-done | bytes 262160 | tf_op jit(solution)/shard_map/reduce_scatter | solution.py:113
  270.4 1.8 divide_convert_fusion
  272.3 0.7 add.179
  273.0 16.2 %all-gather.5.cloned.1.call-done = bf16[1024,512]{1,0:T(8,128)(2,1)} async-done(((bf16[256,512]{1,0:T(8,128)(2,1)}), bf16[1024,512]{1,0:T(8,128)(2,1)}) %all-gather.5.cloned.1.call-update) | async-done | bytes 1048592 | tf_op jit(solution)/shard_map/all_gather | solution.py:120
  289.1 2.3 copy.58
  (52 shorter events, 2.0 us)
Async XLA Ops:
  8.5 1.6 copy-start
  15.0 7.6 %copy-start.4 = (bf16[1024,512]{1,0:T(8,128)(2,1)S(1)}, bf16[1024,512]{1,0:T(8,128)(2,1)}, u32[]{:S(2)}) copy-start(bf16[1024,512]{1,0:T(8,128)(2,1)} %param.4) | copy-start | bytes 3145732
  15.0 112.0 %all-to-all-start = ((bf16[4,8,9,16,512]{4,3,2,0,1:T(8,128)(2,1)}), bf16[4,8,9,16,512]{4,3,2,0,1:T(8,128)(2,1)}, u32[]{:S(2)}, u32[]{:S(2)}) async-start(bf16[4,8,9,16,512]{4,3,2,0,1:T(8,128)(2,1)} %copy.32), calls=%async_computation | async-start | bytes 9437184 | tf_op jit(solution)/shard_map/all_to_all | solution.py:89
  129.8 2.1 copy-start.1
  131.9 2.2 copy-start.2
  135.8 10.2 %all-to-all-start.1 = ((f32[8,1,576]{2,1,0:T(1,128)}), f32[8,1,576]{2,1,0:T(1,128)S(1)}, u32[]{:S(2)}, u32[]{:S(2)}) async-start(f32[8,1,576]{2,1,0:T(1,128)} %reshape.375), calls=%async_computation.1 | async-start | bytes 40960 | tf_op jit(solution)/shard_map/all_to_all | solution.py:95
  139.4 49.6 %reduce-scatter.3.cloned.1.call-start = ((), (), s32[]{:S(2)}) async-start(), calls=%async_computation.7 | async-start | bytes 1310720 | tf_op jit(solution)/shard_map/reduce_scatter | solution.py:113
  160.5 6.4 %copy-start.5 = (u32[32]{0:T(128)S(1)}, u32[32]{0:T(128)}, u32[]{:S(2)}) copy-start(u32[32]{0:T(128)} %constant.79) | copy-start | bytes 388
  166.8 41.1 %all-gather.3.cloned.1.call-start = ((), (), s32[]{:S(2)}) async-start(), calls=%async_computation.8 | async-start | bytes 1310720 | tf_op jit(solution)/shard_map/all_gather | solution.py:120
  190.8 79.6 %reduce-scatter.5.cloned.1.call-start = ((), (), s32[]{:S(2)}) async-start(), calls=%async_computation.9 | async-start | bytes 1310720 | tf_op jit(solution)/shard_map/reduce_scatter | solution.py:113
  213.7 2.2 copy-start.3
  249.1 40.1 %all-gather.5.cloned.1.call-start = ((), (), s32[]{:S(2)}) async-start(), calls=%async_computation.10 | async-start | bytes 1310720 | tf_op jit(solution)/shard_map/all_gather | solution.py:120
Sparse Core Ops, SparseCore 0:
  166.9 22.0 reduce-scatter.2
  191.2 16.6 all-gather.2
  249.2 21.1 reduce-scatter.4
  272.4 16.6 all-gather.4

commit v3 on v2

--- a/solution.py
+++ b/solution.py
@@ -1,3 +1,4 @@
+import functools
 import math
 
 import jax
@@ -33,6 +34,58 @@
         out_specs=vmem,
         compiler_params=pltpu.CompilerParams(vmem_limit_bytes=32 << 20),
     )(home_block, grouped)
+
+
+def swap_kernel(parts, x, out, landed, send_sem, recv_sem):
+    me = lax.axis_index("pts")
+    barrier = pltpu.get_barrier_semaphore()
+    for step in range(1, parts):
+        pl.semaphore_signal(
+            barrier, inc=1, device_id={"pts": lax.rem(me + step, parts)},
+            device_id_type=pl.DeviceIdType.MESH,
+        )
+    pl.semaphore_wait(barrier, parts - 1)
+    copies = []
+    for step in range(1, parts):
+        peer = lax.rem(me + step, parts)
+        copy = pltpu.make_async_remote_copy(
+            src_ref=x.at[peer],
+            dst_ref=landed.at[me],
+            send_sem=send_sem.at[step],
+            recv_sem=recv_sem.at[step],
+            device_id={"pts": peer},
+            device_id_type=pl.DeviceIdType.MESH,
+        )
+        copy.start()
+        copies.append(copy)
+    out[me] = x[me]
+    for step in range(1, parts):
+        copies[step - 1].wait()
+        origin = lax.rem(me - step + parts, parts)
+        out[origin] = landed[origin]
+
+
+def swap(values, number):
+    held, owners, capacity, width = values.shape
+    size = held * capacity * width
+    full = -(-size // 1024) * 1024
+    flat = jnp.swapaxes(values, 0, 1).reshape(owners, size)
+    flat = jnp.pad(flat, ((0, 0), (0, full - size))).reshape(owners, full // 128, 128)
+    vmem = pl.BlockSpec(memory_space=pltpu.VMEM)
+    result = pl.pallas_call(
+        functools.partial(swap_kernel, owners),
+        out_shape=jax.ShapeDtypeStruct(flat.shape, flat.dtype),
+        in_specs=[vmem],
+        out_specs=vmem,
+        scratch_shapes=[
+            pltpu.VMEM(flat.shape, flat.dtype),
+            pltpu.SemaphoreType.DMA((owners,)),
+            pltpu.SemaphoreType.DMA((owners,)),
+        ],
+        compiler_params=pltpu.CompilerParams(collective_id=number, has_side_effects=True),
+    )(flat)
+    result = result.reshape(owners, full)[:, :size]
+    return jnp.swapaxes(result.reshape(owners, held, capacity, width), 0, 1)
 
 
 def make_scoring(centre_table, centre_norms, inverse_root):
@@ -92,13 +145,13 @@
         centre_norms = jnp.sum(jnp.square(centre_table.astype(jnp.float32)), axis=2)
         scoring = make_scoring(centre_table, centre_norms, inverse_root)
         scores, partial_value = scoring(arrived)
-        returned = lax.all_to_all(partial_value, "pts", split_axis=1, concat_axis=1, tiled=True)
+        returned = swap(partial_value, 2 * iteration)
         per_entry = returned.reshape(slot_count, PB)[position]
         paired = per_entry.reshape(point_blocks, 2, PB)
         point_lse = stable_lse(paired, 1)
         outward = jnp.where(filled[:, None], point_lse[home_block], jnp.float32(1e30))
         outward = outward.reshape(slot_shape + (PB,))
-        inward = lax.all_to_all(outward, "pts", split_axis=1, concat_axis=1, tiled=True)
+        inward = swap(outward, 2 * iteration + 1)
         weights = jnp.exp(scores - inward[..., None])
         leading = weights.shape[0]
         flat_weights = weights.reshape(leading, -1, CB)

time: 299 us -> 298 us (level)
  Pallas kernels: 2.22 us -> 34 us
  blocking collectives: 41.3 us -> 11.6 us
  local copies, waits for them, and re-layouts: 24.6 us -> 28.7 us
  starting transfers between devices: 11.4 us -> 7.78 us
  other arithmetic: 17.2 us -> 14.1 us
    pallas_call x0 -> x4, Pallas kernels: none -> 31.8 us  [swap(): pl.pallas_call(functools.partial(swap_kernel, owners), out_shape=jax.Shap...]
    all_to_all x3 -> x0, blocking collectives: 29.9 us -> none  [the longest x2 17.9 us: on_device(): lax.all_to_all(outward, 'pts', split_axis=1, concat_axis=1, tiled=True)]
    all_to_all x1 -> x0, waiting for transfers between devices: 6.43 us -> none  [on_device(): lax.all_to_all(partial_value, 'pts', split_axis=1, concat_axis=1, tiled=T...]
    reduce_scatter x2, waiting for transfers between devices: 24.1 us -> 30 us  [on_device(): lax.psum_scatter(weighted, 'cent', scatter_dimension=0, tiled=True)]
    unnamed x25 -> x29, local copies, waits for them, and re-layouts: 11.8 us -> 15.6 us
    all_to_all x1 -> x0, starting transfers between devices: 3.64 us -> none  [on_device(): lax.all_to_all(partial_value, 'pts', split_axis=1, concat_axis=1, tiled=T...]
  transfers between devices with their start and end apart: 6 -> 5, of which waited for: 6 -> 5; matrix products, arithmetic and copies ran while one was open for 3% -> 3% of each run, Pallas kernels for 0% -> 0%
where the time goes in v3:
time: 298 us; the launch traced here: 297 us
  waiting for transfers between devices  167 us (56%)
  Pallas kernels  34 us (11%)
  local copies, waits for them, and re-layouts  28.7 us (10%)
  matrix products  18.7 us (6%)
  between operations  14.8 us (5%)
  other arithmetic  14.1 us (5%)
  blocking collectives  11.6 us (4%)
  starting transfers between devices  7.78 us (3%)
    all_to_all x1, waiting for transfers between devices, on_device(): lax.all_to_all(outgoing, 'pts', split_axis=1, concat_axis=1, tiled=True)  104 us
    all_gather x2, waiting for transfers between devices, on_device(): current = lax.all_gather(renewed, 'cent', axis=0, tiled=True)  33 us
    pallas_call x4, Pallas kernels, swap(): pl.pallas_call(functools.partial(swap_kernel, owners), out_shape=jax.Shap...  31.8 us
    reduce_scatter x2, waiting for transfers between devices, on_device(): lax.psum_scatter(weighted, 'cent', scatter_dimension=0, tiled=True)  30 us
    unnamed x29, local copies, waits for them, and re-layouts  15.6 us
    dot_general x2, matrix products, on_device(): jnp.einsum('lsm,lsd->lmd', rounded, flat_rows, preferred_element_type=jnp...  12.6 us
    unnamed x2, blocking collectives  11.6 us
    all_to_all x1, starting transfers between devices, on_device(): lax.all_to_all(outgoing, 'pts', split_axis=1, concat_axis=1, tiled=True)  7.44 us
  transfers between devices with their start and end apart: 5, of which 5 were waited for; matrix products, arithmetic and copies ran while one was open for 3% of the time, Pallas kernels for 0%

profile of v3, /device:TPU:0, one launch (start us, length us, event | category | flops | bytes accessed | tf_op | source)
XLA Modules:
  0.0 296.6 jit_solution(13038729645586399382)
XLA Ops:
  7.2 0.8 copy.43
  7.9 0.1 reshape.367
  8.1 0.2 fusion.20
  8.3 0.1 select_reduce_fusion
  8.5 1.6 copy-done
  10.1 2.2 shard_map.50
  12.3 2.7 copy.44
  15.0 7.4 %all-to-all-start = ((bf16[4,8,9,16,512]{4,3,2,0,1:T(8,128)(2,1)}), bf16[4,8,9,16,512]{4,3,2,0,1:T(8,128)(2,1)}, u32[]{:S(2)}, u32[]{:S(2)}) async-start(bf16[4,8,9,16,512]{4,3,2,0,1:T(8,128)(2,1)} %copy.44), calls=%async_computation | async-start | bytes 9437184 | tf_op jit(solution)/shard_map/all_to_all | solution.py:142
  22.5 0.1 reshape.377
  22.6 0.3 multiply_reduce_fusion.1
  23.1 103.8 %all-to-all-done = bf16[4,8,9,16,512]{4,3,2,0,1:T(8,128)(2,1)} async-done(((bf16[4,8,9,16,512]{4,3,2,0,1:T(8,128)(2,1)}), bf16[4,8,9,16,512]{4,3,2,0,1:T(8,128)(2,1)}, u32[]{:S(2)}, u32[]{:S(2)}) %all-to-all-start) | async-done | bytes 4718624 | tf_op jit(solution)/shard_map/all_to_all | solution.py:142
  127.0 2.8 copy.45
  129.8 1.7 fusion.30
  131.5 0.4 copy-done.1
  131.9 2.2 copy-done.2
  134.1 0.6 exponential_reduce_fusion.1
  134.9 0.1 reshape.372
  135.1 0.6 copy.88
  135.7 7.8 %shard_map.51 = f32[8,8,128]{2,1,0:T(8,128)} custom-call(f32[8,8,128]{2,1,0:T(8,128)} %bitcast.92), custom_call_target="tpu_custom_call" | custom-call | tf_op jit(solution)/shard_map/pallas_call | solution.py:75
  143.5 0.8 copy.87
  144.5 0.7 gather_fusion
  145.2 0.2 reduce_max.37
  145.4 0.2 exponential_reduce_fusion.3
  145.6 1.1 gather_fusion.1
  146.8 0.3 gather.18
  147.1 0.3 copy.51
  147.5 0.6 copy.86
  148.2 7.9 %shard_map.52 = f32[8,8,128]{2,1,0:T(8,128)} custom-call(f32[8,8,128]{2,1,0:T(8,128)} %bitcast.94), custom_call_target="tpu_custom_call" | custom-call | tf_op jit(solution)/shard_map/pallas_call | solution.py:75
  156.0 0.8 copy.85
  156.9 0.1 sub.108
  157.1 6.3 %fusion.14 = bf16[4,256,512]{2,1,0:T(8,128)(2,1)} fusion(bf16[4,1152,512]{2,1,0:T(8,128)(2,1)} %bitcast.75, f32[4,1152,256]{1,2,0:T(8,128)} %copy-done.2, f32[4,1152]{1,0:T(4,128)S(1)} %sub.108), kind=kOutput, calls=%fused_computation.24 | convolution fusion | flops 1210843136 | bytes 10504192 | tf_op jit(solution)/shard_map/lsm,lsd->lmd/dot_general | solution.py:161
  163.5 0.6 dynamic-slice
  164.7 3.0 %fusion.4 = f32[4,256]{1,0:T(4,128)S(1)} fusion(f32[4,1152,256]{1,2,0:T(8,128)} %copy-done.2, f32[4,1152]{1,0:T(4,128)S(1)} %sub.108), kind=kLoop, calls=%fused_computation.14 | loop fusion | flops 2358272 | bytes 4741120 | tf_op jit(solution)/shard_map/reduce_sum | solution.py:158
  167.7 5.7 %all-reduce.4 = f32[1024]{0:T(1024)S(1)} all-reduce(f32[1024]{0:T(1024)S(1)} %bitcast.106), channel_id=3, replica_groups=mesh['pts'=8,'cent'=4] {'cent'}, use_global_device_ids=true, to_apply=%region_9.10.clone | all-reduce | flops 1024 | bytes 8192
  173.5 14.3 %reduce-scatter.3.cloned.1.call-done = bf16[256,512]{1,0:T(8,128)(2,1)} async-done(((bf16[1024,512]{1,0:T(8,128)(2,1)}), bf16[256,512]{1,0:T(8,128)(2,1)}) %reduce-scatter.3.cloned.1.call-update) | async-done | bytes 262160 | tf_op jit(solution)/shard_map/reduce_scatter | solution.py:166
  187.7 1.8 divide_convert_fusion.1
  189.5 0.2 reduce-scatter.5.cloned.1.call-start
  189.8 16.9 %all-gather.3.cloned.1.call-done = bf16[1024,512]{1,0:T(8,128)(2,1)} async-done(((bf16[256,512]{1,0:T(8,128)(2,1)}), bf16[1024,512]{1,0:T(8,128)(2,1)}) %all-gather.3.cloned.1.call-update) | async-done | bytes 1048592 | tf_op jit(solution)/shard_map/all_gather | solution.py:173
  206.6 1.5 multiply_reduce_fusion
  208.1 4.2 %fusion.31 = (f32[4,1152]{1,0:T(4,128)S(1)}, f32[4,1152,256]{1,2,0:T(8,128)S(1)}) fusion(f32[4,256]{1,0:T(4,128)S(1)} %sub.111, bf16[4,1152,512]{2,1,0:T(8,128)(2,1)} %bitcast.76, bf16[4,256,512]{2,1,0:T(8,128)(2,1)} %bitcast.81), kind=kOutput, calls=%fused_computation.87 | convolution fusion | flops 1212673536 | bytes 10508288 | tf_op jit(solution)/shard_map/lsd,lmd->lsm/dot_general | solution.py:97
  212.4 2.2 copy-done.3
  214.6 0.6 exponential_reduce_fusion
  215.4 0.1 reshape.386
  215.5 0.6 copy.84
  216.1 8.1 %shard_map.53 = f32[8,8,128]{2,1,0:T(8,128)} custom-call(f32[8,8,128]{2,1,0:T(8,128)} %bitcast.96), custom_call_target="tpu_custom_call" | custom-call | tf_op jit(solution)/shard_map/pallas_call | solution.py:75
  224.2 0.8 copy.83
  225.1 0.7 gather_fusion.2
  225.9 0.2 reduce_max.39
  226.0 0.2 exponential_reduce_fusion.2
  226.3 1.1 gather_fusion.3
  227.5 0.3 gather.21
  227.8 0.3 copy.57
  228.2 0.6 copy.82
  228.8 8.0 %shard_map.54 = f32[8,8,128]{2,1,0:T(8,128)} custom-call(f32[8,8,128]{2,1,0:T(8,128)} %bitcast.98), custom_call_target="tpu_custom_call" | custom-call | tf_op jit(solution)/shard_map/pallas_call | solution.py:75
  236.9 0.8 copy.81
  237.8 0.1 sub.118
  237.9 6.3 %fusion.17 = bf16[4,256,512]{2,1,0:T(8,128)(2,1)} fusion(bf16[4,1152,512]{2,1,0:T(8,128)(2,1)} %bitcast.77, f32[4,1152,256]{1,2,0:T(8,128)} %copy-done.3, f32[4,1152]{1,0:T(4,128)S(1)} %sub.118), kind=kOutput, calls=%fused_computation.25 | convolution fusion | flops 1210843136 | bytes 10504192 | tf_op jit(solution)/shard_map/lsm,lsd->lmd/dot_general | solution.py:161
  244.3 3.0 %fusion.6 = f32[4,256]{1,0:T(4,128)S(1)} fusion(f32[4,1152,256]{1,2,0:T(8,128)} %copy-done.3, f32[4,1152]{1,0:T(4,128)S(1)} %sub.118), kind=kLoop, calls=%fused_computation.16 | loop fusion | flops 2358272 | bytes 4741120 | tf_op jit(solution)/shard_map/reduce_sum | solution.py:158
  247.3 5.9 %all-reduce.5 = f32[1024]{0:T(1024)S(1)} all-reduce(f32[1024]{0:T(1024)S(1)} %bitcast.107), channel_id=5, replica_groups=mesh['pts'=8,'cent'=4] {'cent'}, use_global_device_ids=true, to_apply=%region_17.18.clone | all-reduce | flops 1024 | bytes 8192
  253.3 15.7 %reduce-scatter.5.cloned.1.call-done = bf16[256,512]{1,0:T(8,128)(2,1)} async-done(((bf16[1024,512]{1,0:T(8,128)(2,1)}), bf16[256,512]{1,0:T(8,128)(2,1)}) %reduce-scatter.5.cloned.1.call-update) | async-done | bytes 262160 | tf_op jit(solution)/shard_map/reduce_scatter | solution.py:166
  269.1 1.8 divide_convert_fusion
  270.9 0.7 add.197
  271.6 16.2 %all-gather.5.cloned.1.call-done = bf16[1024,512]{1,0:T(8,128)(2,1)} async-done(((bf16[256,512]{1,0:T(8,128)(2,1)}), bf16[1024,512]{1,0:T(8,128)(2,1)}) %all-gather.5.cloned.1.call-update) | async-done | bytes 1048592 | tf_op jit(solution)/shard_map/all_gather | solution.py:173
  287.8 2.3 copy.90
  (62 shorter events, 2.0 us)
Async XLA Ops:
  8.5 1.6 copy-start
  15.0 7.6 %copy-start.4 = (bf16[1024,512]{1,0:T(8,128)(2,1)S(1)}, bf16[1024,512]{1,0:T(8,128)(2,1)}, u32[]{:S(2)}) copy-start(bf16[1024,512]{1,0:T(8,128)(2,1)} %param.4) | copy-start | bytes 3145732
  15.0 112.0 %all-to-all-start = ((bf16[4,8,9,16,512]{4,3,2,0,1:T(8,128)(2,1)}), bf16[4,8,9,16,512]{4,3,2,0,1:T(8,128)(2,1)}, u32[]{:S(2)}, u32[]{:S(2)}) async-start(bf16[4,8,9,16,512]{4,3,2,0,1:T(8,128)(2,1)} %copy.44), calls=%async_computation | async-start | bytes 9437184 | tf_op jit(solution)/shard_map/all_to_all | solution.py:142
  22.4 165.3 %reduce-scatter.3.cloned.1.call-start = ((), (), s32[]{:S(2)}) async-start(), calls=%async_computation.3 | async-start | bytes 1310720 | tf_op jit(solution)/shard_map/reduce_scatter | solution.py:166
  129.8 2.1 copy-start.1
  131.9 2.2 copy-start.2
  157.1 6.4 %copy-start.5 = (u32[32]{0:T(128)S(1)}, u32[32]{0:T(128)}, u32[]{:S(2)}) copy-start(u32[32]{0:T(128)} %constant.88) | copy-start | bytes 388
  163.4 43.2 %all-gather.3.cloned.1.call-start = ((), (), s32[]{:S(2)}) async-start(), calls=%async_computation.4 | async-start | bytes 1310720 | tf_op jit(solution)/shard_map/all_gather | solution.py:173
  189.5 79.5 %reduce-scatter.5.cloned.1.call-start = ((), (), s32[]{:S(2)}) async-start(), calls=%async_computation.5 | async-start | bytes 1310720 | tf_op jit(solution)/shard_map/reduce_scatter | solution.py:166
  212.4 2.2 copy-start.3
  244.2 43.6 %all-gather.5.cloned.1.call-start = ((), (), s32[]{:S(2)}) async-start(), calls=%async_computation.6 | async-start | bytes 1310720 | tf_op jit(solution)/shard_map/all_gather | solution.py:173
Sparse Core Ops, SparseCore 0:
  163.5 24.1 reduce-scatter.2
  189.9 16.6 all-gather.2
  244.3 24.6 reduce-scatter.4
  271.1 16.6 all-gather.4
